TPU v7x, 32 devices: a whole 2x2x4 slice. The times are simulated.
32 devices in a mesh: groups: 2 (over y), ctx: 4 (over z), role: 2 (over x), seq: 2 (over core).
Axes of the slice: x: 2, y: 2, z: 4, core: 2. Of those that a mesh axis runs over, the one named last changes fastest.
Arguments:
- queries: bfloat16 [32, 128, 576], P(('groups', 'role', 'seq'), 'ctx'), parts along dimension 0, may hold values from -24 to 24
- cache: bfloat16 [16, 4096, 576], P(('groups', 'role', 'seq'), 'ctx'), parts along dimension 0, may hold values from -4 to 4
- lengths: int32 [16], P(('groups', 'role', 'seq')), parts along dimension 0, may hold values from 4 to 4096, as said below
- positions: int32 [32], P(('groups', 'role', 'seq')), parts along dimension 0, may hold values from 0 to 4098, as said below
- value_up_weight: bfloat16 [128, 512, 128], P('ctx', ('role', 'seq')), may hold values from -0.25 to 0.25
- out_proj: bfloat16 [16384, 7168], P('ctx', ('role', 'seq')), may hold values from -0.046875 to 0.046875
- residual: bfloat16 [32, 7168], P('groups', ('role', 'seq')), parts along dimension 0, may hold values from -4 to 4
- norm_gain: float32 [7168], P(('role', 'seq')), may hold values from 0.5 to 1.5
- gate_weight: bfloat16 [7168, 9216], P(('role', 'seq'), 'ctx'), may hold values from -0.0625 to 0.0625
- up_weight: bfloat16 [7168, 9216], P(('role', 'seq'), 'ctx'), may hold values from -0.0625 to 0.0625
- down_weight: bfloat16 [9216, 7168], P('ctx', ('role', 'seq')), may hold values from -0.0625 to 0.0625
Outputs:
- layer_out: bfloat16 [32, 7168], P(('groups', 'ctx'), ('role', 'seq')), parts along dimension 0
There are 2 independent parts, one for each index of `groups`. A program takes and returns all parts, laid end to end along the dimension named above; an argument that names none is the same for every part. Nothing has to cross between parts.
Inputs may be any that keep to these rules, and one draw needn't show every extreme that they name: `lengths`: every sequence has at least 4 cached positions, and in every draw some sequence has all 4096. positions[r] lies between lengths[r // 2] - 4 and lengths[r // 2] + 2.
All inputs are finite; a program needn't handle non-finite values.
Results may differ from a plain program's by a relative error of at most 0.013.
Values may be sent and summed in bfloat16 or wider, within the bound.
A program may use at most 128 MiB of HBM per device.

v0:
```python
import jax
import jax.numpy as jnp
from jax import lax
from jax.sharding import PartitionSpec as P

D = 7168
HEADS = 128
LATENT = 512
ROPE = 64
VDIM = 128
MTP = 2
softmax_scale = 0.07216878364870323
epsilon = 1e-06


def settle_heads(pieces):
    maxima, totals, partial_value = pieces
    highest = jnp.max(maxima, axis=0)
    factor = jnp.exp(maxima - highest[None])
    denom = jnp.sum(factor * totals, axis=0)
    numer = jnp.sum(factor[..., None] * partial_value, axis=0)
    return (numer / denom[..., None]).astype(jnp.bfloat16)


def per_device(
    queries,
    cache,
    lengths,
    positions,
    value_up_weight,
    out_proj,
    residual,
    norm_gain,
    gate_weight,
    up_weight,
    down_weight,
):
    all_heads = lax.all_gather(queries, "ctx", axis=1, tiled=True)
    heads_here = queries.shape[1]
    width = LATENT + ROPE
    context_local = cache.shape[1]
    seq_here = cache.shape[0]
    offset = lax.axis_index("ctx") * context_local
    places = offset + jnp.arange(context_local, dtype=jnp.int32)
    maxima_list = []
    totals_list = []
    partial_list = []
    for number in range(seq_here):
        rows_pair = all_heads[MTP * number : MTP * (number + 1)].reshape(MTP * HEADS, width)
        keys_here = cache[number]
        limits = jnp.repeat(positions[MTP * number : MTP * (number + 1)], HEADS)
        length = lengths[number]

        def compute_block(rows_pair=rows_pair, keys_here=keys_here, limits=limits, length=length):
            scores = (
                jnp.dot(rows_pair, keys_here.T, preferred_element_type=jnp.float32) * softmax_scale
            )
            live = (places[None, :] < length) & (places[None, :] <= limits[:, None])
            block_max = jnp.max(jnp.where(live, scores, jnp.float32(-1e30)), axis=-1)
            probs = jnp.exp(
                jnp.where(live, scores - block_max[:, None], jnp.float32(-1e30))
            ).astype(jnp.bfloat16)
            block_weight_sum = jnp.sum(probs.astype(jnp.float32), axis=-1)
            block_out = jnp.dot(probs, keys_here[:, :LATENT], preferred_element_type=jnp.float32)
            return (block_max, block_weight_sum, block_out)

        block_max, block_weight_sum, block_out = compute_block()
        maxima_list.append(block_max.reshape(MTP, HEADS))
        totals_list.append(block_weight_sum.reshape(MTP, HEADS))
        partial_list.append(block_out.reshape(MTP, HEADS, LATENT))
    maxima = jnp.concatenate(maxima_list, axis=0)
    totals = jnp.concatenate(totals_list, axis=0)
    partial_value = jnp.concatenate(partial_list, axis=0)
    attended_values = settle_heads(
        (
            lax.all_to_all(maxima[None], "ctx", split_axis=2, concat_axis=0, tiled=True),
            lax.all_to_all(totals[None], "ctx", split_axis=2, concat_axis=0, tiled=True),
            lax.all_to_all(partial_value[None], "ctx", split_axis=2, concat_axis=0, tiled=True),
        )
    )
    mixed = jnp.einsum(
        "nut,utc->nuc",
        attended_values,
        lax.all_gather(value_up_weight, ("role", "seq"), axis=1, tiled=True),
        preferred_element_type=jnp.float32,
    )
    value_vectors = mixed.astype(jnp.bfloat16).reshape(attended_values.shape[0], heads_here * VDIM)
    per_head_terms = jnp.dot(
        lax.all_gather(value_vectors, ("role", "seq"), axis=0, tiled=True),
        out_proj,
        preferred_element_type=jnp.float32,
    )
    attn_out = lax.psum(per_head_terms, "ctx")
    resid = residual.astype(jnp.float32) + attn_out
    sumsq = lax.psum(jnp.sum(resid * resid, axis=1), ("role", "seq"))
    normed = (resid * lax.rsqrt(sumsq / D + epsilon)[:, None] * norm_gain[None, :]).astype(
        jnp.bfloat16
    )
    gate_term = jnp.dot(normed, gate_weight, preferred_element_type=jnp.float32)
    up_term = jnp.dot(normed, up_weight, preferred_element_type=jnp.float32)
    gate, up = lax.psum((gate_term, up_term), ("role", "seq"))
    hidden = (jax.nn.silu(gate) * up).astype(jnp.bfloat16)
    rows_here = resid.shape[0] // lax.axis_size("ctx")
    ffn_rows = lax.psum_scatter(
        jnp.dot(hidden, down_weight, preferred_element_type=jnp.float32),
        "ctx",
        scatter_dimension=0,
        tiled=True,
    )
    base_rows = lax.dynamic_slice_in_dim(resid, lax.axis_index("ctx") * rows_here, rows_here, 0)
    return (base_rows + ffn_rows).astype(jnp.bfloat16)


def solution(mesh):
    placed = (
        P(("groups", "role", "seq"), "ctx", None),
        P(("groups", "role", "seq"), "ctx", None),
        P(("groups", "role", "seq")),
        P(("groups", "role", "seq")),
        P("ctx", ("role", "seq"), None),
        P("ctx", ("role", "seq")),
        P("groups", ("role", "seq")),
        P(("role", "seq")),
        P(("role", "seq"), "ctx"),
        P(("role", "seq"), "ctx"),
        P("ctx", ("role", "seq")),
    )
    return jax.shard_map(
        per_device,
        mesh=mesh,
        in_specs=placed,
        out_specs=P(("groups", "ctx"), ("role", "seq")),
        check_vma=False,
    )
```

profile of v0, /device:TPU:0, one launch (start us, length us, event | category | flops | bytes accessed | tf_op | source)
XLA Modules:
  0.0 227.1 jit_solution(11326140525146923370)
XLA Ops:
  6.5 0.0 all-gather.3.cloned.1.call-start
  6.5 0.7 all-gather.3.cloned.1.call-update
  7.3 1.3 fusion.19
  8.6 1.3 fusion.12
  9.9 19.9 %all_gather.9 = bf16[4,128,576]{2,1,0:T(8,128)(2,1)S(1)} all-gather(bf16[4,32,576]{2,1,0:T(8,128)(2,1)} %param.11), channel_id=1, replica_groups=mesh['groups'=2,'ctx'=4,'role'=2,'seq'=2] {'ctx'}, dimensions={1}, use_global_device_ids=true | all-gather | bytes 737280 | tf_op jit(solution)/shard_map/all_gather | solution.py:38
  29.8 0.8 fusion.20
  30.6 0.1 broadcast_bitcast_fusion
  30.7 0.1 fusion.18
  30.7 1.8 convolution_multiply_fusion
  32.6 0.0 copy-done
  32.6 0.9 select_reduce_fusion.1
  33.5 0.9 convert_reduce_fusion.1
  34.4 0.1 copy.23
  34.5 0.6 broadcast.49
  35.1 0.8 reduce.1
  35.9 0.7 reshape.68
  36.6 3.8 %all-to-all-start.2 = ((f32[4,1,128]{2,1,0:T(1,128)}), f32[4,1,128]{2,1,0:T(1,128)S(1)}, u32[]{:S(2)}, u32[]{:S(2)}) async-start(f32[4,1,128]{2,1,0:T(1,128)} %reshape.68), calls=%async_computation.2 | async-start | bytes 4096 | tf_op jit(solution)/shard_map/all_to_all | solution.py:77
  40.4 0.2 slice_bitcast_fusion.1
  40.6 0.5 fusion.3
  41.1 0.5 fusion.1
  41.6 0.1 copy.18
  41.7 0.8 reduce.3
  42.5 0.7 reshape.66
  43.2 0.4 copy.20
  43.6 0.4 copy.21
  44.0 1.9 all-to-all-done.2
  45.9 3.2 %all-to-all-start = ((f32[4,1,128]{2,1,0:T(1,128)}), f32[4,1,128]{2,1,0:T(1,128)S(1)}, u32[]{:S(2)}, u32[]{:S(2)}) async-start(f32[4,1,128]{2,1,0:T(1,128)} %reshape.66), calls=%async_computation | async-start | bytes 4096 | tf_op jit(solution)/shard_map/all_to_all | solution.py:76
  49.1 1.4 maximum_bitcast_fusion
  50.6 4.1 %all-to-all-done = f32[4,1,128]{2,1,0:T(1,128)S(1)} async-done(((f32[4,1,128]{2,1,0:T(1,128)}), f32[4,1,128]{2,1,0:T(1,128)S(1)}, u32[]{:S(2)}, u32[]{:S(2)}) %all-to-all-start) | async-done | bytes 2080 | tf_op jit(solution)/shard_map/all_to_all | solution.py:76
  54.7 3.5 %all-to-all-start.1 = ((f32[1,4,128,512]{3,1,0,2:T(4,128)}), f32[1,4,128,512]{3,1,0,2:T(4,128)S(1)}, u32[]{:S(2)}, u32[]{:S(2)}) async-start(f32[1,4,128,512]{3,1,0,2:T(4,128)} %maximum_bitcast_fusion), calls=%async_computation.1 | async-start | bytes 2097152 | tf_op jit(solution)/shard_map/all_to_all | solution.py:78
  58.2 0.0 all-reduce.6.cloned.1.call-start
  58.3 0.7 reduce.2
  58.9 0.1 reshape.69
  59.1 0.1 copy.24
  59.2 0.7 reduce.4
  59.8 0.1 reshape.67
  60.0 0.1 copy.19
  60.1 18.8 %all-to-all-done.1 = f32[1,4,128,512]{3,1,0,2:T(4,128)S(1)} async-done(((f32[1,4,128,512]{3,1,0,2:T(4,128)}), f32[1,4,128,512]{3,1,0,2:T(4,128)S(1)}, u32[]{:S(2)}, u32[]{:S(2)}) %all-to-all-start.1) | async-done | bytes 1048608 | tf_op jit(solution)/shard_map/all_to_all | solution.py:78
  78.9 0.3 fusion.5
  79.3 0.1 divide_convert_fusion
  79.4 0.0 all-gather.3.cloned.1.call-done
  79.4 2.8 %fusion = bf16[1,4,4096]{2,1,0:T(4,128)(2,1)S(1)} fusion(bf16[32,512,128]{2,1,0:T(8,128)(2,1)} %all-gather.3.cloned.1.call-done, bf16[4,32,512]{2,1,0:T(8,128)(2,1)S(1)} %divide_convert_fusion), kind=kOutput, calls=%fused_computation.5 | convolution fusion | flops 16793600 | bytes 4358144 | tf_op jit(solution)/shard_map/nut,utc->nuc/dot_general | solution.py:81
  82.2 5.4 %all-gather = bf16[4,4,4096]{2,1,0:T(4,128)(2,1)S(1)} all-gather(bf16[1,4,4096]{2,1,0:T(4,128)(2,1)S(1)} %fusion), channel_id=1, replica_groups=mesh['groups'=2,'ctx'=4,'role'=2,'seq'=2] {'role','seq'}, dimensions={0}, use_global_device_ids=true | all-gather | bytes 163840 | tf_op jit(solution)/shard_map/all_gather | solution.py:89
  87.7 0.0 copy-start.2
  87.7 0.0 copy-start.1
  87.7 7.8 %fusion.21 = f32[16,1792]{1,0:T(8,128)} fusion(bf16[16,4096]{1,0:T(8,128)(2,1)S(1)} %reshape.63, bf16[4096,1792]{1,0:T(8,128)(2,1)} %param.16), kind=kOutput, calls=%fused_computation.50 | convolution fusion | flops 234881024 | bytes 14925824 | tf_op jit(solution)/shard_map/dot_general | solution.py:88
  95.5 0.0 all-reduce.6.cloned.1.call-update
  95.6 0.0 all-reduce.10.cloned.1.call-start
  95.6 33.5 %all-reduce.6.cloned.1.call-done = f32[16,1792]{1,0:T(8,128)} async-done(((f32[16,1792]{1,0:T(8,128)}), f32[16,1792]{1,0:T(8,128)}) %all-reduce.6.cloned.1.call-update) | async-done | bytes 114704 | tf_op jit(solution)/shard_map/psum | solution.py:93
  129.1 0.0 copy-done.2
  129.1 1.0 multiply_reduce_fusion
  130.1 5.7 %psum.29 = f32[16]{0:T(128)S(1)} all-reduce(f32[16]{0:T(128)S(1)} %get-tuple-element.9), channel_id=1, replica_groups=mesh['groups'=2,'ctx'=4,'role'=2,'seq'=2] {'role','seq'}, use_global_device_ids=true, to_apply=%region_9.10 | all-reduce | flops 16 | bytes 128 | tf_op jit(solution)/shard_map/psum | solution.py:95
  135.8 0.0 copy-done.1
  135.8 5.2 %fusion.16 = f32[16,2304]{1,0:T(8,128)} fusion(bf16[1792,2304]{1,0:T(8,128)(2,1)} %param.19, f32[16,1792]{1,0:T(8,128)S(1)} %get-tuple-element.10, f32[1792]{0:T(1024)S(1)} %copy-done.1, f32[16]{0:T(128)S(1)} %add_rsqrt_fusion), kind=kOutput, calls=%fused_computation.46 | convolution fusion | flops 132206592 | bytes 8526912 | tf_op jit(solution)/shard_map/dot_general | solution.py:99
  141.1 5.3 %fusion.15 = f32[16,2304]{1,0:T(8,128)} fusion(bf16[1792,2304]{1,0:T(8,128)(2,1)} %param.20, f32[16,1792]{1,0:T(8,128)S(1)} %get-tuple-element.10, f32[1792]{0:T(1024)S(1)} %copy-done.1, f32[16]{0:T(128)S(1)} %add_rsqrt_fusion), kind=kOutput, calls=%fused_computation.45 | convolution fusion | flops 132206592 | bytes 8526912 | tf_op jit(solution)/shard_map/dot_general | solution.py:100
  146.3 0.0 all-reduce.10.cloned.1.call-update
  146.3 0.0 all-reduce.8.cloned.1.call-start
  146.4 32.9 %all-reduce.10.cloned.1.call-done = (f32[16,2304]{1,0:T(8,128)}, f32[16,2304]{1,0:T(8,128)}) async-done(((f32[16,2304]{1,0:T(8,128)}, f32[16,2304]{1,0:T(8,128)}), (f32[16,2304]{1,0:T(8,128)}, f32[16,2304]{1,0:T(8,128)})) %all-reduce.10.cloned.1.call-update) | async-done | bytes 294928 | tf_op jit(solution)/shard_map/psum | solution.py:101
  179.2 5.4 %fusion.7 = f32[16,1792]{1,0:T(8,128)} fusion(bf16[2304,1792]{1,0:T(8,128)(2,1)} %param.21, f32[16,2304]{1,0:T(8,128)} %get-tuple-element.7, f32[16,2304]{1,0:T(8,128)} %get-tuple-element.8), kind=kOutput, calls=%fused_computation.27 | convolution fusion | flops 132341760 | bytes 8667136 | tf_op jit(solution)/shard_map/dot_general | solution.py:105
  184.6 0.0 all-reduce.8.cloned.1.call-update
  184.7 0.0 copy-done.3
  184.7 0.6 dynamic-slice
  185.9 33.3 %all-reduce.8.cloned.1.call-done = f32[16,1792]{1,0:T(8,128)} async-done(((f32[16,1792]{1,0:T(8,128)}), f32[16,1792]{1,0:T(8,128)}) %all-reduce.8.cloned.1.call-update) | async-done | bytes 114704
  219.2 1.4 fusion.9
  (9 shorter events, 0.1 us)
Async XLA Ops:
  6.5 26.1 %copy-start = (bf16[2,1024,576]{1,2,0:T(8,128)(2,1)S(1)}, bf16[2,1024,576]{1,2,0:T(8,128)(2,1)}, u32[]{:S(2)}) copy-start(bf16[2,1024,576]{1,2,0:T(8,128)(2,1)} %param.12) | copy-start | bytes 7077892
  6.5 72.8 %all-gather.3.cloned.1.call-start = ((), (), s32[]{:S(2)}) async-start(), calls=%async_computation.3 | async-start | bytes 5242880 | tf_op jit(solution)/shard_map/all_gather | solution.py:84
  36.6 9.3 %all-to-all-start.2 = ((f32[4,1,128]{2,1,0:T(1,128)}), f32[4,1,128]{2,1,0:T(1,128)S(1)}, u32[]{:S(2)}, u32[]{:S(2)}) async-start(f32[4,1,128]{2,1,0:T(1,128)} %reshape.68), calls=%async_computation.2 | async-start | bytes 4096 | tf_op jit(solution)/shard_map/all_to_all | solution.py:77
  45.9 8.8 %all-to-all-start = ((f32[4,1,128]{2,1,0:T(1,128)}), f32[4,1,128]{2,1,0:T(1,128)S(1)}, u32[]{:S(2)}, u32[]{:S(2)}) async-start(f32[4,1,128]{2,1,0:T(1,128)} %reshape.66), calls=%async_computation | async-start | bytes 4096 | tf_op jit(solution)/shard_map/all_to_all | solution.py:76
  54.7 24.2 %all-to-all-start.1 = ((f32[1,4,128,512]{3,1,0,2:T(4,128)}), f32[1,4,128,512]{3,1,0,2:T(4,128)S(1)}, u32[]{:S(2)}, u32[]{:S(2)}) async-start(f32[1,4,128,512]{3,1,0,2:T(4,128)} %maximum_bitcast_fusion), calls=%async_computation.1 | async-start | bytes 2097152 | tf_op jit(solution)/shard_map/all_to_all | solution.py:78
  58.2 70.9 %all-reduce.6.cloned.1.call-start = ((), (), s32[]{:S(2)}) async-start(), calls=%async_computation.4 | async-start | bytes 229376 | tf_op jit(solution)/shard_map/psum | solution.py:93
  87.7 41.4 %copy-start.2 = (bf16[16,1792]{1,0:T(8,128)(2,1)S(1)}, bf16[16,1792]{1,0:T(8,128)(2,1)}, u32[]{:S(2)}) copy-start(bf16[16,1792]{1,0:T(8,128)(2,1)} %param.17) | copy-start | bytes 172036
  87.7 48.1 %copy-start.1 = (f32[1792]{0:T(1024)S(1)}, f32[1792]{0:T(1024)}, u32[]{:S(2)}) copy-start(f32[1792]{0:T(1024)} %param.18) | copy-start | bytes 21508
  95.6 83.7 %all-reduce.10.cloned.1.call-start = ((), (), s32[]{:S(2)}) async-start(), calls=%async_computation.6 | async-start | bytes 589824 | tf_op jit(solution)/shard_map/psum | solution.py:101
  146.3 72.8 %all-reduce.8.cloned.1.call-start = ((), (), s32[]{:S(2)}) async-start(), calls=%async_computation.5 | async-start | bytes 229376
  179.2 5.4 %copy-start.3 = (u32[32]{0:T(128)S(1)}, u32[32]{0:T(128)}, u32[]{:S(2)}) copy-start(u32[32]{0:T(128)} %constant.35) | copy-start | bytes 388
Sparse Core Ops, SparseCore 0:
  8.9 37.1 all-gather.2
  95.7 33.3 all-reduce.5
  146.4 32.7 all-reduce.9
  184.8 34.3 all-reduce.7
where the time goes:
time: 228 us; the launch traced here: 227 us
  waiting for transfers between devices  125 us (55%)
  blocking collectives  31 us (14%)
  matrix products  30.3 us (13%)
  between operations  14 us (6%)
  starting transfers between devices  10.7 us (5%)
  other arithmetic  9.47 us (4%)
  local copies, waits for them, and re-layouts  6.56 us (3%)
    unnamed x5, waiting for transfers between devices  34 us
    psum x1, waiting for transfers between devices, per_device(): attn_out = lax.psum(per_head_terms, 'ctx')  33.5 us
    psum x1, waiting for transfers between devices, per_device(): gate, up = lax.psum((gate_term, up_term), ('role', 'seq'))  32.9 us
    all_gather x1, blocking collectives, per_device(): all_heads = lax.all_gather(queries, 'ctx', axis=1, tiled=True)  19.9 us
    all_to_all x1, waiting for transfers between devices, per_device(): lax.all_to_all(partial_value[None], 'ctx', split_axis=2, concat_axis=0, t...  18.8 us
    dot_general x1, matrix products, per_device(): jnp.dot(lax.all_gather(value_vectors, ('role', 'seq'), axis=0, tiled=True...  7.84 us
    psum x1, blocking collectives, per_device(): sumsq = lax.psum(jnp.sum(resid * resid, axis=1), ('role', 'seq'))  5.66 us
    all_gather x1, blocking collectives, per_device(): lax.all_gather(value_vectors, ('role', 'seq'), axis=0, tiled=True)  5.41 us
  transfers between devices with their start and end apart: 7, of which 6 were waited for; matrix products, arithmetic and copies ran while one was open for 8% of the time, Pallas kernels for 0%

commit v1 on v0

--- a/solution.py
+++ b/solution.py
@@ -1,3 +1,4 @@
+import functools
 import jax
 import jax.numpy as jnp
 from jax import lax
@@ -11,6 +12,25 @@
 MTP = 2
 softmax_scale = 0.07216878364870323
 epsilon = 1e-06
+
+
+def wrap_the_teams(array_here, dev_axis):
+    dev_n = lax.psum(1, axis_name=dev_axis)
+    rack = [(to_i, (to_i + 1) % dev_n) for to_i in range(dev_n)]
+
+    def process_limits(latest):
+        if len(latest) == dev_n:
+            return latest
+        new = lax.ppermute(latest[0], axis_name=dev_axis, perm=rack)
+        return process_limits([new, *latest])
+
+    e_next = process_limits([array_here])
+    frame_out = jnp.concatenate(e_next, axis=1)
+    work_now = lax.axis_index(dev_axis)
+    return jnp.roll(frame_out, (work_now + 1) * array_here.shape[1], axis=1)
+
+
+derive_slots = functools.partial(wrap_the_teams, dev_axis="ctx")
 
 
 def settle_heads(pieces):
@@ -35,7 +55,7 @@
     up_weight,
     down_weight,
 ):
-    all_heads = lax.all_gather(queries, "ctx", axis=1, tiled=True)
+    all_heads = derive_slots(queries)
     heads_here = queries.shape[1]
     width = LATENT + ROPE
     context_local = cache.shape[1]

time: 228 us -> 231 us (1.013)
  blocking collectives: 31 us -> 11.1 us
  waiting for transfers between devices: 125 us -> 141 us
  starting transfers between devices: 10.7 us -> 14.9 us
  local copies, waits for them, and re-layouts: 6.56 us -> 8.93 us
    all_gather x1 -> x0, blocking collectives: 19.9 us -> none  [per_device(): all_heads = lax.all_gather(queries, 'ctx', axis=1, tiled=True)]
    ppermute x0 -> x3, waiting for transfers between devices: none -> 16.8 us  [process_limits(): new = lax.ppermute(latest[0], axis_name=dev_axis, perm=rack)]
    all_to_all x1, waiting for transfers between devices: 4.12 us -> 0.1 us  [per_device(): lax.all_to_all(maxima[None], 'ctx', split_axis=2, concat_axis=0, tiled=True)]
    ppermute x0 -> x3, starting transfers between devices: none -> 3.11 us  [process_limits(): new = lax.ppermute(latest[0], axis_name=dev_axis, perm=rack)]
    unnamed x15 -> x34, local copies, waits for them, and re-layouts: 2.89 us -> 5.05 us
  transfers between devices with their start and end apart: 7 -> 10, of which waited for: 6 -> 9; matrix products, arithmetic and copies ran while one was open for 8% -> 8% of each run, Pallas kernels for 0% -> 0%
where the time goes in v1:
time: 231 us; the launch traced here: 230 us
  waiting for transfers between devices  141 us (61%)
  matrix products  29.9 us (13%)
  starting transfers between devices  14.9 us (6%)
  between operations  14.1 us (6%)
  blocking collectives  11.1 us (5%)
  other arithmetic  10.4 us (5%)
  local copies, waits for them, and re-layouts  8.93 us (4%)
    unnamed x5, waiting for transfers between devices  34 us
    psum x1, waiting for transfers between devices, per_device(): attn_out = lax.psum(per_head_terms, 'ctx')  33 us
    psum x1, waiting for transfers between devices, per_device(): gate, up = lax.psum((gate_term, up_term), ('role', 'seq'))  32.9 us
    all_to_all x1, waiting for transfers between devices, per_device(): lax.all_to_all(partial_value[None], 'ctx', split_axis=2, concat_axis=0, t...  19.9 us
    ppermute x3, waiting for transfers between devices, process_limits(): new = lax.ppermute(latest[0], axis_name=dev_axis, perm=rack)  16.8 us
    dot_general x1, matrix products, per_device(): jnp.dot(lax.all_gather(value_vectors, ('role', 'seq'), axis=0, tiled=True...  7.84 us
    psum x1, blocking collectives, per_device(): sumsq = lax.psum(jnp.sum(resid * resid, axis=1), ('role', 'seq'))  5.66 us
    all_gather x1, blocking collectives, per_device(): lax.all_gather(value_vectors, ('role', 'seq'), axis=0, tiled=True)  5.41 us
  transfers between devices with their start and end apart: 10, of which 9 were waited for; matrix products, arithmetic and copies ran while one was open for 8% of the time, Pallas kernels for 0%

profile of v1, /device:TPU:0, one launch (start us, length us, event | category | flops | bytes accessed | tf_op | source)
XLA Modules:
  0.0 230.1 jit_solution(6211619310496948453)
XLA Ops:
  6.5 0.7 all-gather.3.cloned.1.call-update
  7.3 3.1 %collective-permute-start = (bf16[4,32,576]{2,1,0:T(8,128)(2,1)}, bf16[4,32,576]{2,1,0:T(8,128)(2,1)S(1)}, u32[]{:S(2)}, u32[]{:S(2)}) collective-permute-start(bf16[4,32,576]{2,1,0:T(8,128)(2,1)} %param.11), channel_id=1, source_target_pairs={{0,4},{4,8},{8,12},{12,0},{1,5},{5,9},{9,13},{13,1},{2,6},{6,10},{... | collective-permute-start | bytes 442376 | tf_op jit(solution)/shard_map/ppermute | solution.py:24
  10.4 1.8 slice_bitcast_fusion.1
  12.2 0.1 fusion.19
  12.3 4.5 %collective-permute-done = bf16[4,32,576]{2,1,0:T(8,128)(2,1)S(1)} collective-permute-done((bf16[4,32,576]{2,1,0:T(8,128)(2,1)}, bf16[4,32,576]{2,1,0:T(8,128)(2,1)S(1)}, u32[]{:S(2)}, u32[]{:S(2)}) %collective-permute-start) | collective-permute-done | bytes 147488 | tf_op jit(solution)/shard_map/ppermute | solution.py:24
  16.8 0.1 broadcast_bitcast_fusion
  16.9 0.6 fusion.18
  17.5 6.5 %collective-permute-done.1 = bf16[4,32,576]{2,1,0:T(8,128)(2,1)S(1)} collective-permute-done((bf16[4,32,576]{2,1,0:T(8,128)(2,1)S(1)}, bf16[4,32,576]{2,1,0:T(8,128)(2,1)S(1)}, u32[]{:S(2)}, u32[]{:S(2)}) %collective-permute-start.1) | collective-permute-done | bytes 147488 | tf_op jit(solution)/shard_map/ppermute | solution.py:24
  24.0 1.3 fusion.12
  25.3 5.8 %collective-permute-done.2 = bf16[4,32,576]{2,1,0:T(8,128)(2,1)S(1)} collective-permute-done((bf16[4,32,576]{2,1,0:T(8,128)(2,1)S(1)}, bf16[4,32,576]{2,1,0:T(8,128)(2,1)S(1)}, u32[]{:S(2)}, u32[]{:S(2)}) %collective-permute-start.2) | collective-permute-done | bytes 147488 | tf_op jit(solution)/shard_map/ppermute | solution.py:24
  31.4 0.1 constant_dynamic-slice_fusion
  31.4 1.5 copy-done
  32.9 0.6 convolution_multiply_fusion
  33.5 1.8 select_reduce_fusion.1
  35.3 0.6 copy-done.5
  35.9 0.0 copy-done.6
  35.9 0.1 copy.18
  36.0 0.5 broadcast.50
  36.5 0.7 reduce.3
  37.3 0.7 reshape.66
  38.0 3.2 %all-to-all-start = ((f32[4,1,128]{2,1,0:T(1,128)}), f32[4,1,128]{2,1,0:T(1,128)S(1)}, u32[]{:S(2)}, u32[]{:S(2)}) async-start(f32[4,1,128]{2,1,0:T(1,128)} %reshape.66), calls=%async_computation | async-start | bytes 4096 | tf_op jit(solution)/shard_map/all_to_all | solution.py:96
  41.2 2.1 convert_reduce_fusion.1
  43.3 0.5 fusion.3
  43.7 0.5 fusion.1
  44.2 0.1 copy.23
  44.4 0.7 reduce.1
  45.1 0.7 reshape.68
  45.8 0.4 copy.20
  46.2 0.4 copy.21
  46.6 0.1 all-to-all-done
  46.7 5.0 %all-to-all-start.2 = ((f32[4,1,128]{2,1,0:T(1,128)}), f32[4,1,128]{2,1,0:T(1,128)S(1)}, u32[]{:S(2)}, u32[]{:S(2)}) async-start(f32[4,1,128]{2,1,0:T(1,128)} %reshape.68), calls=%async_computation.2 | async-start | bytes 4096 | tf_op jit(solution)/shard_map/all_to_all | solution.py:97
  51.7 1.4 maximum_bitcast_fusion
  53.1 4.0 %all-to-all-done.2 = f32[4,1,128]{2,1,0:T(1,128)S(1)} async-done(((f32[4,1,128]{2,1,0:T(1,128)}), f32[4,1,128]{2,1,0:T(1,128)S(1)}, u32[]{:S(2)}, u32[]{:S(2)}) %all-to-all-start.2) | async-done | bytes 2080 | tf_op jit(solution)/shard_map/all_to_all | solution.py:97
  57.2 3.5 %all-to-all-start.1 = ((f32[1,4,128,512]{3,1,0,2:T(4,128)}), f32[1,4,128,512]{3,1,0,2:T(4,128)S(1)}, u32[]{:S(2)}, u32[]{:S(2)}) async-start(f32[1,4,128,512]{3,1,0,2:T(4,128)} %maximum_bitcast_fusion), calls=%async_computation.1 | async-start | bytes 2097152 | tf_op jit(solution)/shard_map/all_to_all | solution.py:98
  60.7 0.0 all-reduce.6.cloned.1.call-start
  60.8 0.6 reduce.4
  61.3 0.1 reshape.67
  61.5 0.1 copy.19
  61.6 0.6 reduce.2
  62.2 0.1 reshape.69
  62.3 0.1 copy.24
  62.5 19.9 %all-to-all-done.1 = f32[1,4,128,512]{3,1,0,2:T(4,128)S(1)} async-done(((f32[1,4,128,512]{3,1,0,2:T(4,128)}), f32[1,4,128,512]{3,1,0,2:T(4,128)S(1)}, u32[]{:S(2)}, u32[]{:S(2)}) %all-to-all-start.1) | async-done | bytes 1048608 | tf_op jit(solution)/shard_map/all_to_all | solution.py:98
  82.4 0.3 fusion.5
  82.7 0.1 divide_convert_fusion
  82.8 0.0 all-gather.3.cloned.1.call-done
  82.8 2.8 %fusion = bf16[1,4,4096]{2,1,0:T(4,128)(2,1)S(1)} fusion(bf16[32,512,128]{2,1,0:T(8,128)(2,1)} %all-gather.3.cloned.1.call-done, bf16[4,32,512]{2,1,0:T(8,128)(2,1)S(1)} %divide_convert_fusion), kind=kOutput, calls=%fused_computation.5 | convolution fusion | flops 16793600 | bytes 4358144 | tf_op jit(solution)/shard_map/nut,utc->nuc/dot_general | solution.py:101
  85.7 5.4 %all-gather = bf16[4,4,4096]{2,1,0:T(4,128)(2,1)S(1)} all-gather(bf16[1,4,4096]{2,1,0:T(4,128)(2,1)S(1)} %fusion), channel_id=1, replica_groups=mesh['groups'=2,'ctx'=4,'role'=2,'seq'=2] {'role','seq'}, dimensions={0}, use_global_device_ids=true | all-gather | bytes 163840 | tf_op jit(solution)/shard_map/all_gather | solution.py:109
  91.1 0.0 copy-start.3
  91.1 7.8 %fusion.20 = f32[16,1792]{1,0:T(8,128)} fusion(bf16[16,4096]{1,0:T(8,128)(2,1)S(1)} %reshape.63, bf16[4096,1792]{1,0:T(8,128)(2,1)} %param.16), kind=kOutput, calls=%fused_computation.59 | convolution fusion | flops 234881024 | bytes 14925824 | tf_op jit(solution)/shard_map/dot_general | solution.py:108
  99.0 0.0 all-reduce.6.cloned.1.call-update
  99.0 0.0 all-reduce.10.cloned.1.call-start
  99.0 33.0 %all-reduce.6.cloned.1.call-done = f32[16,1792]{1,0:T(8,128)} async-done(((f32[16,1792]{1,0:T(8,128)}), f32[16,1792]{1,0:T(8,128)}) %all-reduce.6.cloned.1.call-update) | async-done | bytes 114704 | tf_op jit(solution)/shard_map/psum | solution.py:113
  132.1 1.0 multiply_reduce_fusion
  133.1 5.7 %psum.29 = f32[16]{0:T(128)S(1)} all-reduce(f32[16]{0:T(128)S(1)} %get-tuple-element.9), channel_id=1, replica_groups=mesh['groups'=2,'ctx'=4,'role'=2,'seq'=2] {'role','seq'}, use_global_device_ids=true, to_apply=%region_9.10 | all-reduce | flops 16 | bytes 128 | tf_op jit(solution)/shard_map/psum | solution.py:115
  138.8 5.2 %fusion.16 = f32[16,2304]{1,0:T(8,128)} fusion(bf16[1792,2304]{1,0:T(8,128)(2,1)} %param.19, f32[16,1792]{1,0:T(8,128)S(1)} %get-tuple-element.10, f32[1792]{0:T(1024)S(1)} %copy-done.2, f32[16]{0:T(128)S(1)} %add_rsqrt_fusion), kind=kOutput, calls=%fused_computation.56 | convolution fusion | flops 132206592 | bytes 8526912 | tf_op jit(solution)/shard_map/dot_general | solution.py:119
  144.0 5.3 %fusion.15 = f32[16,2304]{1,0:T(8,128)} fusion(bf16[1792,2304]{1,0:T(8,128)(2,1)} %param.20, f32[16,1792]{1,0:T(8,128)S(1)} %get-tuple-element.10, f32[1792]{0:T(1024)S(1)} %copy-done.2, f32[16]{0:T(128)S(1)} %add_rsqrt_fusion), kind=kOutput, calls=%fused_computation.55 | convolution fusion | flops 132206592 | bytes 8526912 | tf_op jit(solution)/shard_map/dot_general | solution.py:120
  149.3 0.0 all-reduce.10.cloned.1.call-update
  149.3 0.0 all-reduce.8.cloned.1.call-start
  149.3 32.9 %all-reduce.10.cloned.1.call-done = (f32[16,2304]{1,0:T(8,128)}, f32[16,2304]{1,0:T(8,128)}) async-done(((f32[16,2304]{1,0:T(8,128)}, f32[16,2304]{1,0:T(8,128)}), (f32[16,2304]{1,0:T(8,128)}, f32[16,2304]{1,0:T(8,128)})) %all-reduce.10.cloned.1.call-update) | async-done | bytes 294928 | tf_op jit(solution)/shard_map/psum | solution.py:121
  182.2 5.4 %fusion.7 = f32[16,1792]{1,0:T(8,128)} fusion(bf16[2304,1792]{1,0:T(8,128)(2,1)} %param.21, f32[16,2304]{1,0:T(8,128)} %get-tuple-element.7, f32[16,2304]{1,0:T(8,128)} %get-tuple-element.8), kind=kOutput, calls=%fused_computation.27 | convolution fusion | flops 132341760 | bytes 8667136 | tf_op jit(solution)/shard_map/dot_general | solution.py:125
  187.6 0.0 all-reduce.8.cloned.1.call-update
  187.6 0.6 dynamic-slice
  188.9 33.3 %all-reduce.8.cloned.1.call-done = f32[16,1792]{1,0:T(8,128)} async-done(((f32[16,1792]{1,0:T(8,128)}), f32[16,1792]{1,0:T(8,128)}) %all-reduce.8.cloned.1.call-update) | async-done | bytes 114704
  222.1 1.4 fusion.9
  (34 shorter events, 0.3 us)
Async XLA Ops:
  6.5 76.3 %all-gather.3.cloned.1.call-start = ((), (), s32[]{:S(2)}) async-start(), calls=%async_computation.3 | async-start | bytes 5242880 | tf_op jit(solution)/shard_map/all_gather | solution.py:104
  7.3 5.0 %copy-start.7 = (s32[4]{0:T(128)S(1)}, s32[4]{0:T(128)}, u32[]{:S(2)}) copy-start(s32[4]{0:T(128)} %param.14) | copy-start | bytes 52
  7.3 9.6 %copy-start.8 = (s32[2]{0:T(128)S(1)}, s32[2]{0:T(128)}, u32[]{:S(2)}) copy-start(s32[2]{0:T(128)} %param.13) | copy-start | bytes 28
  7.3 23.9 %copy-start.1 = (bf16[4,32,576]{2,1,0:T(8,128)(2,1)S(1)}, bf16[4,32,576]{2,1,0:T(8,128)(2,1)}, u32[]{:S(2)}) copy-start(bf16[4,32,576]{2,1,0:T(8,128)(2,1)} %param.11) | copy-start | bytes 442372
  7.3 9.5 %collective-permute-start = (bf16[4,32,576]{2,1,0:T(8,128)(2,1)}, bf16[4,32,576]{2,1,0:T(8,128)(2,1)S(1)}, u32[]{:S(2)}, u32[]{:S(2)}) collective-permute-start(bf16[4,32,576]{2,1,0:T(8,128)(2,1)} %param.11), channel_id=1, source_target_pairs={{0,4},{4,8},{8,12},{12,0},{1,5},{5,9},{9,13},{13,1},{2,6},{6,10},{... | collective-permute-start | bytes 442376 | tf_op jit(solution)/shard_map/ppermute | solution.py:24
  16.8 7.2 %collective-permute-start.1 = (bf16[4,32,576]{2,1,0:T(8,128)(2,1)S(1)}, bf16[4,32,576]{2,1,0:T(8,128)(2,1)S(1)}, u32[]{:S(2)}, u32[]{:S(2)}) collective-permute-start(bf16[4,32,576]{2,1,0:T(8,128)(2,1)S(1)} %collective-permute-done), channel_id=1, source_target_pairs={{0,4},{4,8},{8,12},{12,0},{1,5},{5,9},{9,13},{13,1},{2,6},{6,10},{... | collective-permute-start | bytes 442376 | tf_op jit(solution)/shard_map/ppermute | solution.py:24
  24.0 7.1 %collective-permute-start.2 = (bf16[4,32,576]{2,1,0:T(8,128)(2,1)S(1)}, bf16[4,32,576]{2,1,0:T(8,128)(2,1)S(1)}, u32[]{:S(2)}, u32[]{:S(2)}) collective-permute-start(bf16[4,32,576]{2,1,0:T(8,128)(2,1)S(1)} %collective-permute-done.1), channel_id=1, source_target_pairs={{0,4},{4,8},{8,12},{12,0},{1,5},{5,9},{9,13},{13,1},{2,6},{6,10},{... | collective-permute-start | bytes 442376 | tf_op jit(solution)/shard_map/ppermute | solution.py:24
  25.3 8.2 %copy-start.4 = (pred[1024]{0:T(1024)(128)(4,1)}, pred[1024]{0:T(1024)(128)(4,1)S(1)}, u32[]{:S(2)}) copy-start(pred[1024]{0:T(1024)(128)(4,1)S(1)} %get-tuple-element.29) | copy-start | bytes 3076
  31.2 1.7 copy-start
  35.3 0.6 copy-start.5
  35.3 0.6 copy-start.6
  38.0 8.7 %all-to-all-start = ((f32[4,1,128]{2,1,0:T(1,128)}), f32[4,1,128]{2,1,0:T(1,128)S(1)}, u32[]{:S(2)}, u32[]{:S(2)}) async-start(f32[4,1,128]{2,1,0:T(1,128)} %reshape.66), calls=%async_computation | async-start | bytes 4096 | tf_op jit(solution)/shard_map/all_to_all | solution.py:96
  46.7 10.5 %all-to-all-start.2 = ((f32[4,1,128]{2,1,0:T(1,128)}), f32[4,1,128]{2,1,0:T(1,128)S(1)}, u32[]{:S(2)}, u32[]{:S(2)}) async-start(f32[4,1,128]{2,1,0:T(1,128)} %reshape.68), calls=%async_computation.2 | async-start | bytes 4096 | tf_op jit(solution)/shard_map/all_to_all | solution.py:97
  57.2 25.2 %all-to-all-start.1 = ((f32[1,4,128,512]{3,1,0,2:T(4,128)}), f32[1,4,128,512]{3,1,0,2:T(4,128)S(1)}, u32[]{:S(2)}, u32[]{:S(2)}) async-start(f32[1,4,128,512]{3,1,0,2:T(4,128)} %maximum_bitcast_fusion), calls=%async_computation.1 | async-start | bytes 2097152 | tf_op jit(solution)/shard_map/all_to_all | solution.py:98
  60.7 71.3 %all-reduce.6.cloned.1.call-start = ((), (), s32[]{:S(2)}) async-start(), calls=%async_computation.4 | async-start | bytes 229376 | tf_op jit(solution)/shard_map/psum | solution.py:113
  91.1 40.9 %copy-start.3 = (bf16[16,1792]{1,0:T(8,128)(2,1)S(1)}, bf16[16,1792]{1,0:T(8,128)(2,1)}, u32[]{:S(2)}) copy-start(bf16[16,1792]{1,0:T(8,128)(2,1)} %param.17) | copy-start | bytes 172036
  91.1 47.6 %copy-start.2 = (f32[1792]{0:T(1024)S(1)}, f32[1792]{0:T(1024)}, u32[]{:S(2)}) copy-start(f32[1792]{0:T(1024)} %param.18) | copy-start | bytes 21508
  99.0 83.2 %all-reduce.10.cloned.1.call-start = ((), (), s32[]{:S(2)}) async-start(), calls=%async_computation.6 | async-start | bytes 589824 | tf_op jit(solution)/shard_map/psum | solution.py:121
  149.3 72.8 %all-reduce.8.cloned.1.call-start = ((), (), s32[]{:S(2)}) async-start(), calls=%async_computation.5 | async-start | bytes 229376
  182.2 5.4 %copy-start.9 = (u32[32]{0:T(128)S(1)}, u32[32]{0:T(128)}, u32[]{:S(2)}) copy-start(u32[32]{0:T(128)} %constant.60) | copy-start | bytes 388
Sparse Core Ops, SparseCore 0:
  8.9 37.1 all-gather.2
  99.1 32.8 all-reduce.5
  149.4 32.7 all-reduce.9
  187.7 34.3 all-reduce.7
